TPU v7x, 512 devices: a whole 4x4x16 slice. The times are simulated.
512 devices in a mesh: ea: 4 (over y), row: 16 (over z), col: 8 (over x, core).
Axes of the slice: x: 4, y: 4, z: 16, core: 2. Of those that a mesh axis runs over, the one named last changes fastest.
Arguments:
- weights: float32 [4, 1024, 2048], P('ea', 'row', 'col'), parts along dimension 0, may hold values from -6 to 6
- codebook: float32 [4, 16, 2, 256], P('ea', 'col'), parts along dimension 0, may hold values from -4 to 4
- assign: int32 [4, 1024, 1024], P('ea', 'row', 'col'), parts along dimension 0, may hold values from 0 to 255
- chol_upper: float32 [4, 2048, 2048], P('ea', 'row', 'col'), parts along dimension 0, may hold values from 0 to 1.4, as said below
- inv_blocks: float32 [4, 16, 128, 128], P('ea', 'col'), parts along dimension 0, may hold values from -1 to 1.5, as said below
Outputs:
- errors: float32 [4, 1024, 2048], P('ea', 'row', 'col'), parts along dimension 0
- row_loss: float32 [4, 1024], P('ea', 'row'), parts along dimension 0
- codeword_mass: float32 [4, 16, 256], P('ea', 'col'), parts along dimension 0
There are 4 independent parts, one for each index of `ea`. A program takes and returns all parts, laid end to end along the dimension named above; each array names one. Nothing has to cross between parts.
Inputs may be any that keep to these rules, and one draw needn't show every extreme that they name: `chol_upper`: upper triangular with a positive diagonal. inv_blocks[x, b] is the inverse of the diagonal block of chol_upper[x] on rows and columns [b * 128, (b + 1) * 128).
All inputs are finite; a program needn't handle non-finite values.
Results may differ from a plain program's by a relative error of at most 0.0001.
Values sent between devices are 32-bit elements; how exact they have to be, the bound alone decides.
A program may use at most 64 MiB of HBM per device.

v0:
```python
import jax
import jax.numpy as jnp
from jax import lax
from jax.sharding import PartitionSpec as P


def sent_to_all(value, axis):
    copies = jnp.broadcast_to(value, (lax.axis_size(axis), *value.shape))
    return lax.all_to_all(copies, axis, split_axis=0, concat_axis=0, tiled=True)


def joined_along(parts, dim):
    parts = jnp.moveaxis(parts, 0, dim)
    shape = parts.shape
    return parts.reshape(*shape[:dim], shape[dim] * shape[dim + 1], *shape[dim + 2 :])


def collect(value, axis, dim):
    parts = sent_to_all(value, axis)
    return joined_along(parts, dim)


def picked_2(value, axis, root):
    return lax.dynamic_index_in_dim(lax.all_gather(value, axis), root, 0, keepdims=False)


def of_everyone(value, axis):
    everything = sent_to_all(value, axis)
    return jnp.sum(everything, axis=0)


def flat_labels(assign, half_block, code_count):
    pair_count = assign.shape[2]
    offsets = jnp.arange(pair_count, dtype=jnp.int32) // half_block * code_count
    return assign + offsets[None, None, :]


def lookup_local(codebook, labels):
    experts, row_count, pair_count = labels.shape
    code_table = jnp.transpose(codebook, (0, 2, 1, 3)).reshape(experts, 2, -1)

    def select(rows_table, indices):
        return jnp.stack(
            [jnp.take(rows_table[0], indices), jnp.take(rows_table[1], indices)], axis=-1
        )

    picked = jax.vmap(select)(code_table, labels)
    return picked.reshape(experts, row_count, 2 * pair_count)


def mass_by_code(errors, labels, local_blocks, code_count):
    experts, row_count, width = errors.shape
    squared = errors * errors
    paired = squared.reshape(experts, row_count, width // 2, 2).sum(axis=3)

    def summed(values, marks):
        return jax.ops.segment_sum(
            values.reshape(-1), marks.reshape(-1), num_segments=local_blocks * code_count
        )

    return jax.vmap(summed)(paired, labels).reshape(experts, local_blocks, code_count)


def local(weights, codebook, assign, chol_upper, inv_blocks):
    block_size = inv_blocks.shape[2]
    local_blocks = inv_blocks.shape[1]
    local_width = weights.shape[2]
    code_count = codebook.shape[3]
    column_rank = lax.axis_index("col")
    block_total = local_blocks * lax.axis_size("col")
    labels = flat_labels(assign, block_size // 2, code_count)
    quantized = lookup_local(codebook, labels)
    column_ids = column_rank * local_width + jnp.arange(local_width, dtype=jnp.int32)
    stacked = collect(chol_upper, "row", 1)

    def panel_of(number):
        return lax.dynamic_slice_in_dim(stacked, number * block_size, block_size, 1)

    def own_block(current, number):
        return lax.dynamic_slice_in_dim(current, number % local_blocks * block_size, block_size, 2)

    def block_error(current_block, number):
        owner_rank = number // local_blocks
        inverse = lax.dynamic_index_in_dim(inv_blocks, number % local_blocks, 1, keepdims=False)
        target = own_block(quantized, number)

        def compute():
            return jnp.einsum(
                "xrc,xcd->xrd", current_block - target, inverse, precision=lax.Precision.HIGHEST
            )

        def nothing():
            return jnp.zeros(current_block.shape, jnp.float32)

        computed = lax.cond(owner_rank == column_rank, compute, nothing)
        return picked_2(computed, "col", owner_rank)

    def propagate(current, error_block, panel_rows, number, targets):
        beyond = targets >= (number + 1) * block_size
        masked = jnp.where(beyond[None, None, :], panel_rows, 0.0)
        return current - jnp.einsum(
            "xrc,xcd->xrd", error_block, masked, precision=lax.Precision.HIGHEST
        )

    def record(errors, error_block, number):
        owner_rank = number // local_blocks
        offset = number % local_blocks * block_size
        previous = lax.dynamic_slice_in_dim(errors, offset, block_size, 2)
        chosen = jnp.where(owner_rank == column_rank, error_block, previous)
        return lax.dynamic_update_slice_in_dim(errors, chosen, offset, 2)

    blank = jnp.zeros(weights.shape, jnp.float32)

    def advance(number, state_pair):
        current, errors = state_pair
        error_block = block_error(own_block(current, number), number)
        errors = record(errors, error_block, number)
        current = propagate(current, error_block, panel_of(number), number, column_ids)
        return (current, errors)

    current, errors = lax.fori_loop(0, block_total, advance, (weights, blank))
    row_loss = lax.psum(jnp.sum(errors * errors, axis=2), "col")
    local_mass = mass_by_code(errors, labels, local_blocks, code_count)
    codeword_mass = of_everyone(local_mass, "row")
    return (errors, row_loss, codeword_mass)


def solution(mesh):
    return jax.shard_map(
        local,
        mesh=mesh,
        in_specs=(
            P("ea", "row", "col"),
            P("ea", "col", None, None),
            P("ea", "row", "col"),
            P("ea", "row", "col"),
            P("ea", "col", None, None),
        ),
        out_specs=(P("ea", "row", "col"), P("ea", "row"), P("ea", "col", None)),
        check_vma=False,
    )
```

profile of v0, /device:TPU:7, one launch (start us, length us, event | category | flops | bytes accessed | tf_op | source)
XLA Modules:
  0.0 410.0 jit_solution(16363121114288031070)
XLA Ops:
  0.6 2.5 broadcast_in_dim.53
  3.1 15.0 %all-to-all-start = ((f32[16,1,128,256]{3,2,1,0:T(8,128)}), f32[16,1,128,256]{3,2,1,0:T(8,128)S(1)}, u32[]{:S(2)}, u32[]{:S(2)}) async-start(f32[16,1,128,256]{3,2,1,0:T(8,128)} %broadcast_in_dim.53), calls=%async_computation | async-start | bytes 4194304 | tf_op jit(solution)/shard_map/all_to_all | solution.py:9
  18.2 48.0 %gather_fusion = f32[8192]{0:T(1024)S(1)} fusion(f32[1,512]{1,0:T(1,128)S(1)} %get-tuple-element.348, s32[8192]{0:T(1024)S(1)} %fusion.22), kind=kCustom, calls=%fused_computation.clone | custom fusion | bytes 131072 | tf_op jit(solution)/shard_map/vmap(jit(_take))/gather | solution.py:44
  66.3 48.0 %gather_fusion.1 = f32[8192]{0:T(1024)S(1)} fusion(f32[1,512]{1,0:T(1,128)S(1)} %get-tuple-element.347, s32[8192]{0:T(1024)S(1)} %fusion.22), kind=kCustom, calls=%fused_computation.1.clone | custom fusion | bytes 131072 | tf_op jit(solution)/shard_map/vmap(jit(_take))/gather | solution.py:44
  114.9 211.7 %while.18 = (s32[]{:T(128)}, f32[1,64,256]{2,1,0:T(8,128)S(1)}, f32[1,64,256]{2,1,0:T(8,128)S(1)}, s32[]{:T(128)}, f32[1,64,256]{2,1,0:T(8,128)S(1)}, /*index=5*...) while((s32[]{:T(128)}, f32[1,64,256]{2,1,0:T(8,128)S(1)}, ...), condition=%wide.region_3.5_spmd.clone, body=%wide.region_0.0_spmd.clone.sunk | while | flops 37814816 | bytes 853267 | solution.py:121
  115.0 13.6 %all-gather.3 = f32[8,64,128]{2,1,0:T(8,128)S(1)} all-gather(f32[1,64,128]{2,1,0:T(8,128)S(1)} %get-tuple-element.446), channel_id=2, replica_groups=mesh['ea'=4,'row'=16,'col'=8] {'col'}, dimensions={0}, use_global_device_ids=true | all-gather | bytes 294912 | tf_op jit(solution)/shard_map/while/body/eval_jaxpr/all_gather | solution.py:24
  128.9 12.8 %all-gather.3 = f32[8,64,128]{2,1,0:T(8,128)S(1)} all-gather(f32[1,64,128]{2,1,0:T(8,128)S(1)} %get-tuple-element.446), channel_id=2, replica_groups=mesh['ea'=4,'row'=16,'col'=8] {'col'}, dimensions={0}, use_global_device_ids=true | all-gather | bytes 294912 | tf_op jit(solution)/shard_map/while/body/eval_jaxpr/all_gather | solution.py:24
  142.1 12.8 %all-gather.3 = f32[8,64,128]{2,1,0:T(8,128)S(1)} all-gather(f32[1,64,128]{2,1,0:T(8,128)S(1)} %get-tuple-element.446), channel_id=2, replica_groups=mesh['ea'=4,'row'=16,'col'=8] {'col'}, dimensions={0}, use_global_device_ids=true | all-gather | bytes 294912 | tf_op jit(solution)/shard_map/while/body/eval_jaxpr/all_gather | solution.py:24
  155.2 12.8 %all-gather.3 = f32[8,64,128]{2,1,0:T(8,128)S(1)} all-gather(f32[1,64,128]{2,1,0:T(8,128)S(1)} %get-tuple-element.446), channel_id=2, replica_groups=mesh['ea'=4,'row'=16,'col'=8] {'col'}, dimensions={0}, use_global_device_ids=true | all-gather | bytes 294912 | tf_op jit(solution)/shard_map/while/body/eval_jaxpr/all_gather | solution.py:24
  168.4 12.8 %all-gather.3 = f32[8,64,128]{2,1,0:T(8,128)S(1)} all-gather(f32[1,64,128]{2,1,0:T(8,128)S(1)} %get-tuple-element.446), channel_id=2, replica_groups=mesh['ea'=4,'row'=16,'col'=8] {'col'}, dimensions={0}, use_global_device_ids=true | all-gather | bytes 294912 | tf_op jit(solution)/shard_map/while/body/eval_jaxpr/all_gather | solution.py:24
  181.5 12.8 %all-gather.3 = f32[8,64,128]{2,1,0:T(8,128)S(1)} all-gather(f32[1,64,128]{2,1,0:T(8,128)S(1)} %get-tuple-element.446), channel_id=2, replica_groups=mesh['ea'=4,'row'=16,'col'=8] {'col'}, dimensions={0}, use_global_device_ids=true | all-gather | bytes 294912 | tf_op jit(solution)/shard_map/while/body/eval_jaxpr/all_gather | solution.py:24
  194.7 12.8 %all-gather.3 = f32[8,64,128]{2,1,0:T(8,128)S(1)} all-gather(f32[1,64,128]{2,1,0:T(8,128)S(1)} %get-tuple-element.446), channel_id=2, replica_groups=mesh['ea'=4,'row'=16,'col'=8] {'col'}, dimensions={0}, use_global_device_ids=true | all-gather | bytes 294912 | tf_op jit(solution)/shard_map/while/body/eval_jaxpr/all_gather | solution.py:24
  207.8 12.8 %all-gather.3 = f32[8,64,128]{2,1,0:T(8,128)S(1)} all-gather(f32[1,64,128]{2,1,0:T(8,128)S(1)} %get-tuple-element.446), channel_id=2, replica_groups=mesh['ea'=4,'row'=16,'col'=8] {'col'}, dimensions={0}, use_global_device_ids=true | all-gather | bytes 294912 | tf_op jit(solution)/shard_map/while/body/eval_jaxpr/all_gather | solution.py:24
  221.0 12.8 %all-gather.3 = f32[8,64,128]{2,1,0:T(8,128)S(1)} all-gather(f32[1,64,128]{2,1,0:T(8,128)S(1)} %get-tuple-element.446), channel_id=2, replica_groups=mesh['ea'=4,'row'=16,'col'=8] {'col'}, dimensions={0}, use_global_device_ids=true | all-gather | bytes 294912 | tf_op jit(solution)/shard_map/while/body/eval_jaxpr/all_gather | solution.py:24
  234.1 12.8 %all-gather.3 = f32[8,64,128]{2,1,0:T(8,128)S(1)} all-gather(f32[1,64,128]{2,1,0:T(8,128)S(1)} %get-tuple-element.446), channel_id=2, replica_groups=mesh['ea'=4,'row'=16,'col'=8] {'col'}, dimensions={0}, use_global_device_ids=true | all-gather | bytes 294912 | tf_op jit(solution)/shard_map/while/body/eval_jaxpr/all_gather | solution.py:24
  247.3 12.8 %all-gather.3 = f32[8,64,128]{2,1,0:T(8,128)S(1)} all-gather(f32[1,64,128]{2,1,0:T(8,128)S(1)} %get-tuple-element.446), channel_id=2, replica_groups=mesh['ea'=4,'row'=16,'col'=8] {'col'}, dimensions={0}, use_global_device_ids=true | all-gather | bytes 294912 | tf_op jit(solution)/shard_map/while/body/eval_jaxpr/all_gather | solution.py:24
  260.4 12.8 %all-gather.3 = f32[8,64,128]{2,1,0:T(8,128)S(1)} all-gather(f32[1,64,128]{2,1,0:T(8,128)S(1)} %get-tuple-element.446), channel_id=2, replica_groups=mesh['ea'=4,'row'=16,'col'=8] {'col'}, dimensions={0}, use_global_device_ids=true | all-gather | bytes 294912 | tf_op jit(solution)/shard_map/while/body/eval_jaxpr/all_gather | solution.py:24
  273.6 13.1 %all-gather.3 = f32[8,64,128]{2,1,0:T(8,128)S(1)} all-gather(f32[1,64,128]{2,1,0:T(8,128)S(1)} %get-tuple-element.446), channel_id=2, replica_groups=mesh['ea'=4,'row'=16,'col'=8] {'col'}, dimensions={0}, use_global_device_ids=true | all-gather | bytes 294912 | tf_op jit(solution)/shard_map/while/body/eval_jaxpr/all_gather | solution.py:24
  287.0 13.1 %all-gather.3 = f32[8,64,128]{2,1,0:T(8,128)S(1)} all-gather(f32[1,64,128]{2,1,0:T(8,128)S(1)} %get-tuple-element.446), channel_id=2, replica_groups=mesh['ea'=4,'row'=16,'col'=8] {'col'}, dimensions={0}, use_global_device_ids=true | all-gather | bytes 294912 | tf_op jit(solution)/shard_map/while/body/eval_jaxpr/all_gather | solution.py:24
  300.6 12.6 %all-gather.3 = f32[8,64,128]{2,1,0:T(8,128)S(1)} all-gather(f32[1,64,128]{2,1,0:T(8,128)S(1)} %get-tuple-element.446), channel_id=2, replica_groups=mesh['ea'=4,'row'=16,'col'=8] {'col'}, dimensions={0}, use_global_device_ids=true | all-gather | bytes 294912 | tf_op jit(solution)/shard_map/while/body/eval_jaxpr/all_gather | solution.py:24
  313.8 12.6 %all-gather.3 = f32[8,64,128]{2,1,0:T(8,128)S(1)} all-gather(f32[1,64,128]{2,1,0:T(8,128)S(1)} %get-tuple-element.446), channel_id=2, replica_groups=mesh['ea'=4,'row'=16,'col'=8] {'col'}, dimensions={0}, use_global_device_ids=true | all-gather | bytes 294912 | tf_op jit(solution)/shard_map/while/body/eval_jaxpr/all_gather | solution.py:24
  327.1 57.0 %scatter_custom_fusion = f32[512]{0:T(512)S(1)} fusion(s32[8192]{0:T(1024)S(1)} %broadcast_select_fusion, f32[8192]{0:T(1024)S(1)} %bitcast.66, f32[]{:T(128)} %constant.173.clone.1), kind=kCustom, calls=%fused_computation.48 | custom fusion | flops 8192 | bytes 2052
  384.7 11.7 %all-to-all-start.1 = ((f32[16,1,2,256]{3,2,1,0:T(2,128)}), f32[16,1,2,256]{3,2,1,0:T(2,128)S(1)}, u32[]{:S(2)}, u32[]{:S(2)}) async-start(f32[16,1,2,256]{3,2,1,0:T(2,128)} %broadcast_in_dim.55), calls=%async_computation.1 | async-start | bytes 65536 | tf_op jit(solution)/shard_map/all_to_all | solution.py:9
  396.5 13.0 %psum.7 = f32[1,64]{1,0:T(1,128)} all-reduce(f32[1,64]{1,0:T(1,128)S(1)} %bitcast.69), channel_id=1, replica_groups=mesh['ea'=4,'row'=16,'col'=8] {'col'}, use_global_device_ids=true, to_apply=%region_5.7 | all-reduce | flops 64 | bytes 512 | tf_op jit(solution)/shard_map/psum | solution.py:122
  (117 shorter events, 7.6 us)
Async XLA Ops:
  3.1 15.1 %copy-start.3 = (s32[1,64,128]{2,1,0:T(8,128)S(1)}, s32[1,64,128]{2,1,0:T(8,128)}, u32[]{:S(2)}) copy-start(s32[1,64,128]{2,1,0:T(8,128)} %param.13) | copy-start | bytes 98308
  3.1 15.1 %copy-start.4 = (f32[1,2,2,256]{3,2,1,0:T(2,128)S(1)}, f32[1,2,2,256]{3,2,1,0:T(2,128)}, u32[]{:S(2)}) copy-start(f32[1,2,2,256]{3,2,1,0:T(2,128)} %param.12) | copy-start | bytes 12292
  3.1 111.8 %all-to-all-start = ((f32[16,1,128,256]{3,2,1,0:T(8,128)}), f32[16,1,128,256]{3,2,1,0:T(8,128)S(1)}, u32[]{:S(2)}, u32[]{:S(2)}) async-start(f32[16,1,128,256]{3,2,1,0:T(8,128)} %broadcast_in_dim.53), calls=%async_computation | async-start | bytes 4194304 | tf_op jit(solution)/shard_map/all_to_all | solution.py:9
  66.2 48.3 %copy-start.5 = (s32[2]{0:T(128)S(1)}, s32[2]{0:T(128)}, u32[]{:S(2)}) copy-start(s32[2]{0:T(128)} %constant.185) | copy-start | bytes 28
  66.2 48.4 %copy-start.6 = (s32[2]{0:T(128)S(1)}, s32[2]{0:T(128)}, u32[]{:S(2)}) copy-start(s32[2]{0:T(128)} %constant.188) | copy-start | bytes 28
  66.2 48.7 %copy-start = (f32[1,64,256]{2,1,0:T(8,128)S(1)}, f32[1,64,256]{2,1,0:T(8,128)}, u32[]{:S(2)}) copy-start(f32[1,64,256]{2,1,0:T(8,128)} %param.11) | copy-start | bytes 196612
  66.3 48.7 %copy-start.2 = (f32[1,2,128,128]{3,2,1,0:T(8,128)S(1)}, f32[1,2,128,128]{3,2,1,0:T(8,128)}, u32[]{:S(2)}) copy-start(f32[1,2,128,128]{3,2,1,0:T(8,128)} %param.15) | copy-start | bytes 393220
  326.6 83.4 %copy-start.1 = (f32[1,64,256]{2,1,0:T(8,128)}, f32[1,64,256]{2,1,0:T(8,128)S(1)}, u32[]{:S(2)}) copy-start(f32[1,64,256]{2,1,0:T(8,128)S(1)} %get-tuple-element.262) | copy-start | bytes 196612
  384.7 24.7 %all-to-all-start.1 = ((f32[16,1,2,256]{3,2,1,0:T(2,128)}), f32[16,1,2,256]{3,2,1,0:T(2,128)S(1)}, u32[]{:S(2)}, u32[]{:S(2)}) async-start(f32[16,1,2,256]{3,2,1,0:T(2,128)} %broadcast_in_dim.55), calls=%async_computation.1 | async-start | bytes 65536 | tf_op jit(solution)/shard_map/all_to_all | solution.py:9
where the time goes:
time: 413 us; the launch traced here: 410 us
  blocking collectives  219 us (53%)
  local copies, waits for them, and re-layouts  99.5 us (24%)
  other arithmetic  58.6 us (14%)
  starting transfers between devices  26.8 us (6%)
    all_gather x16, blocking collectives, picked_2(): lax.all_gather(value, axis)  206 us
    unnamed x4, other arithmetic  57.4 us
    gather x2, local copies, waits for them, and re-layouts, select(): jnp.take(rows_table[0], indices)  48 us
    gather x1, local copies, waits for them, and re-layouts, select(): jnp.take(rows_table[1], indices)  48 us
    all_to_all x2, starting transfers between devices, sent_to_all(): return lax.all_to_all(copies, axis, split_axis=0, concat_axis=0, tiled=True)  26.8 us
    psum x1, blocking collectives, local(): row_loss = lax.psum(jnp.sum(errors * errors, axis=2), 'col')  13 us
  transfers between devices with their start and end apart: 2, of which 0 were waited for; matrix products, arithmetic and copies ran while one was open for 24% of the time, Pallas kernels for 0%

commit v1 on v0

v1 whole, which is shorter than its diff:
```python
import functools

import jax
import jax.numpy as jnp
from jax import lax
from jax.experimental import pallas as pl
from jax.experimental.pallas import tpu as pltpu
from jax.sharding import PartitionSpec as P

MESH = pl.DeviceIdType.MESH
HI = lax.Precision.HIGHEST
F32 = jnp.float32
BF = jnp.bfloat16


def dot(a, b):
    return jnp.dot(a, b, precision=HI, preferred_element_type=F32)


def pieces(x):
    high = x.astype(BF)
    rest = x - high.astype(F32)
    mid = rest.astype(BF)
    low = (rest - mid.astype(F32)).astype(BF)
    return high, mid, low


def wide_codes(codes, block):
    rows = codes.shape[0]
    place = lax.broadcasted_iota(jnp.int32, (rows, 128), 1) // 2 + block * 64
    return jnp.take_along_axis(codes, place, axis=1)


def looked_up(table, wide):
    rows = wide.shape[0]
    low = jnp.bitwise_and(wide, 127)
    second = lax.broadcasted_iota(jnp.int32, (rows, 128), 1) % 2 == 1

    def from_half(k, half):
        row = table[k : k + 1, half * 128 : half * 128 + 128]
        return jnp.take_along_axis(jnp.broadcast_to(row, (rows, 128)), low, axis=1)

    def from_component(k):
        return jnp.where(wide >= 128, from_half(k, 1), from_half(k, 0))

    return jnp.where(second, from_component(1), from_component(0))


def mass_of(squared, wide):
    rows = squared.shape[0]
    upper = jnp.right_shift(wide, 4)
    lower = jnp.bitwise_and(wide, 15)
    level = lax.broadcasted_iota(jnp.int32, (16, 128), 0)
    left, right = [], []
    for r in range(rows):
        left.append(jnp.where(upper[r : r + 1, :] == level, squared[r : r + 1, :], 0.0))
        right.append(jnp.where(lower[r : r + 1, :] == level, 1.0, 0.0).astype(BF))
    spread = jnp.concatenate(pieces(jnp.concatenate(left, axis=1)), axis=0)
    hot = jnp.concatenate(right, axis=1)
    summed = lax.dot_general(spread, hot, (((1,), (1,)), ((), ())), preferred_element_type=F32)
    table = summed[0:16] + summed[16:32] + summed[32:48]
    lane = lax.broadcasted_iota(jnp.int32, (16, 128), 1)
    pick = jnp.where(lane % 16 == level, 1.0, 0.0)
    repeated = dot(table, pick)
    kept = jnp.where(lane // 16 == level % 8, repeated, 0.0)
    return jnp.concatenate(
        [jnp.sum(kept[0:8], axis=0, keepdims=True), jnp.sum(kept[8:16], axis=0, keepdims=True)],
        axis=0,
    )


def kernel(
    depth, cols,
    w_hbm, c_hbm, a_hbm, u_hbm, i_hbm,
    err_ref, loss_ref, mass_ref,
    wb, ab, cb, ib, u, xs, es, full_a, va, vh, vb, losses, masses,
    local_sem, pre_send, pre_recv, ring_send, ring_recv, side_send, side_recv,
    stage_send, stage_recv, back_send, back_recv, loss_send, loss_recv, mass_send, mass_recv, entered,
):
    z = lax.axis_index("row")
    c = lax.axis_index("col")
    h = lax.rem(c, 2)
    x = c // 2
    other = 1 - h
    partner = c + 1 - 2 * h
    chips = cols // 2
    rows = wb.shape[1]
    up = lax.rem(z + 1, depth)
    down = lax.rem(z + depth - 1, depth)
    far_up, far_down = depth // 2, (depth - 1) // 2

    mine = pl.ds(pl.multiple_of(h * rows, 8), rows)
    theirs = pl.ds(pl.multiple_of(other * rows, 8), rows)
    local = [
        pltpu.make_async_copy(u_hbm.at[0], u.at[h, z], local_sem.at[0]),
        pltpu.make_async_copy(i_hbm.at[0], ib.at[h], local_sem.at[1]),
        pltpu.make_async_copy(c_hbm.at[0], cb.at[h], local_sem.at[2]),
        pltpu.make_async_copy(w_hbm.at[0, mine], wb.at[h], local_sem.at[3]),
        pltpu.make_async_copy(a_hbm.at[0], full_a, local_sem.at[4]),
    ]
    for copy in local:
        copy.start()

    barrier = pltpu.get_barrier_semaphore()
    for to in (up, down):
        pl.semaphore_signal(barrier, inc=1, device_id={"row": to}, device_id_type=MESH)
    for d in range(1, cols):
        pl.semaphore_signal(
            barrier, inc=1, device_id={"col": lax.rem(c + d, cols)}, device_id_type=MESH
        )
    pl.semaphore_wait(barrier, cols + 1)

    def remote(src, dst, send, recv, **to):
        return pltpu.make_async_remote_copy(
            src_ref=src, dst_ref=dst, send_sem=send, recv_sem=recv, device_id=to,
            device_id_type=MESH,
        )

    def needed(b, column):
        return b <= 2 * column

    def ring_copy(b, way, step):
        return remote(
            u.at[h, b], u.at[h, b], ring_send.at[way, step], ring_recv.at[way, step],
            row=(up if way == 0 else down),
        )

    def side_copy(half, b):
        return remote(u.at[half, b], u.at[half, b], side_send.at[b], side_recv.at[b], col=partner)

    local[0].wait()

    @pl.when(needed(z, c))
    def _():
        ring_copy(z, 0, 1).start()
        ring_copy(z, 1, 1).start()
        side_copy(h, z).start()

    local[1].wait()
    local[2].wait()
    local[4].wait()
    pre = [
        remote(ib.at[h], ib.at[h], pre_send.at[0], pre_recv.at[0], col=partner),
        remote(cb.at[h], cb.at[h], pre_send.at[1], pre_recv.at[1], col=partner),
        remote(w_hbm.at[0, theirs], wb.at[h], pre_send.at[2], pre_recv.at[2], col=partner),
        remote(full_a.at[theirs], ab.at[h], pre_send.at[3], pre_recv.at[3], col=partner),
    ]
    for copy in pre:
        copy.start()
    local[3].wait()
    ab[h] = full_a[mine]

    def ring_step(step, carry):
        for way, farthest in ((0, far_up), (1, far_down)):
            b = lax.rem(z + (depth - step if way == 0 else step), depth)

            @pl.when(jnp.logical_and(step > 1, step <= farthest))
            def _():
                pl.semaphore_wait(entered.at[way], 1)

            @pl.when(step < farthest)
            def _():
                pl.semaphore_signal(
                    entered.at[way], inc=1, device_id={"row": up if way == 0 else down},
                    device_id_type=MESH,
                )

            @pl.when(jnp.logical_and(needed(b, c), step <= farthest))
            def _():
                ring_copy(b, way, step).wait_recv()

                @pl.when(step < farthest)
                def _():
                    ring_copy(b, way, step + 1).start()

                side_copy(h, b).start()

        return carry

    lax.fori_loop(1, far_up + 1, ring_step, 0)

    for copy in pre:
        copy.wait_recv()

    for g in range(2):
        for block in range(2):
            wide = wide_codes(ab[g], block)
            part = slice(block * 128, block * 128 + 128)
            xs[g, :, part] = wb[g, :, part] - looked_up(cb[g, block], wide)

    def side_wait(b, carry):
        @pl.when(needed(b, partner))
        def _():
            side_copy(other, b).wait_recv()

        return carry

    lax.fori_loop(0, depth, side_wait, 0)

    base = 4 * x
    zero = jnp.zeros((128, 128), F32)
    for g, out in ((0, va), (1, vb)):
        first, second = ib[g, 0], ib[g, 1]
        between = u[g, base + 2 * g][:, 128:256]
        corner = -dot(first, dot(between, second))
        out[0:128, 0:128] = first
        out[0:128, 128:256] = corner
        out[128:256, 0:128] = zero
        out[128:256, 128:256] = second
    vh[...] = -dot(va[...], dot(u[1, pl.ds(base, 2)].reshape(256, 256), vb[...]))

    def stage_copy(s, d):
        return remote(
            es.at[s], es.at[s], stage_send.at[d], stage_recv.at[s], col=lax.rem(c + 2 * d, cols)
        )

    def absorb(s, carry):
        stage_copy(s, 1).wait_recv()
        for g in range(2):
            panel = u[g, pl.ds(4 * s, 4)].reshape(512, 256)
            both = jnp.concatenate([es[s, 0], es[s, 1]], axis=1)
            xs[g] = xs[g] - dot(both, panel)
        return carry

    lax.fori_loop(0, x, absorb, 0)
    e0 = dot(xs[0], va[...])
    e1 = dot(xs[0], vh[...]) + dot(xs[1], vb[...])
    es[x, 0] = e0
    es[x, 1] = e1
    for d in range(1, chips):

        @pl.when(x + d < chips)
        def _(d=d):
            stage_copy(x, d).start()

    back = remote(es.at[x, other], err_ref.at[0, mine], back_send, back_recv, col=partner)
    back.start()
    err_ref[0, mine, :] = es[x, h]
    back.wait_recv()

    squared = err_ref[0] * err_ref[0]
    sums = lax.dot_general(
        jnp.ones((8, 256), F32), squared, (((1,), (1,)), ((), ())), precision=HI,
        preferred_element_type=F32,
    )
    losses[c] = sums

    def loss_copy(d):
        return remote(
            losses.at[c], losses.at[c], loss_send.at[d], loss_recv.at[c],
            col=lax.rem(c + d, cols),
        )

    for d in range(1, cols):
        loss_copy(d).start()

    for block in range(2):
        wide = wide_codes(full_a[...], block)
        found = mass_of(squared[:, block * 128 : block * 128 + 128], wide)
        masses[z, 2 * block : 2 * block + 2, :] = found

    def mass_copy(d):
        return remote(
            masses.at[z], masses.at[z], mass_send.at[d], mass_recv.at[z],
            row=lax.rem(z + d, depth),
        )

    def mass_start(d, carry):
        mass_copy(d).start()
        return carry

    lax.fori_loop(1, depth, mass_start, 0)

    def loss_wait(d, carry):
        source = lax.rem(c + d, cols)
        remote(
            losses.at[source], losses.at[source], loss_send.at[d], loss_recv.at[source], col=source
        ).wait_recv()
        return carry

    lax.fori_loop(1, cols, loss_wait, 0)
    loss_ref[...] = jnp.sum(losses[...], axis=0)[0:1, :]

    def mass_wait(d, carry):
        source = lax.rem(z + d, depth)
        remote(
            masses.at[source], masses.at[source], mass_send.at[d], mass_recv.at[source], row=source
        ).wait_recv()
        return carry

    lax.fori_loop(1, depth, mass_wait, 0)
    total = jnp.sum(masses[...], axis=0)
    for block in range(2):
        for part in range(2):
            at = 2 * block + part
            mass_ref[0, block : block + 1, part * 128 : part * 128 + 128] = total[at : at + 1, :]

    @pl.when(needed(z, c))
    def _():
        ring_copy(z, 0, 1).wait_send()
        ring_copy(z, 1, 1).wait_send()
        side_copy(h, z).wait_send()

    def ring_drain(step, carry):
        for way, farthest in ((0, far_up), (1, far_down)):
            b = lax.rem(z + (depth - step if way == 0 else step), depth)

            @pl.when(jnp.logical_and(needed(b, c), step <= farthest))
            def _():
                @pl.when(step < farthest)
                def _():
                    ring_copy(b, way, step + 1).wait_send()

                side_copy(h, b).wait_send()

        return carry

    lax.fori_loop(1, far_up + 1, ring_drain, 0)
    for copy in pre:
        copy.wait_send()
    for d in range(1, chips):

        @pl.when(x + d < chips)
        def _(d=d):
            stage_copy(x, d).wait_send()

    back.wait_send()
    for d in range(1, cols):
        loss_copy(d).wait_send()

    def mass_drain(d, carry):
        mass_copy(d).wait_send()
        return carry

    lax.fori_loop(1, depth, mass_drain, 0)


def local(weights, codebook, assign, chol_upper, inv_blocks):
    depth, cols = lax.axis_size("row"), lax.axis_size("col")
    rows = weights.shape[1] // 2
    hbm = pl.BlockSpec(memory_space=pl.ANY)
    vmem = pl.BlockSpec(memory_space=pltpu.VMEM)
    dma = pltpu.SemaphoreType.DMA
    return tuple(
        pl.pallas_call(
            functools.partial(kernel, depth, cols),
            out_shape=(
                jax.ShapeDtypeStruct(weights.shape, F32),
                jax.ShapeDtypeStruct((1, 2 * rows), F32),
                jax.ShapeDtypeStruct((1, 2, 256), F32),
            ),
            in_specs=[hbm] * 5,
            out_specs=(vmem, vmem, vmem),
            scratch_shapes=[
                pltpu.VMEM((2, rows, 256), F32),
                pltpu.VMEM((2, rows, 128), jnp.int32),
                pltpu.VMEM((2, 2, 2, 256), F32),
                pltpu.VMEM((2, 2, 128, 128), F32),
                pltpu.VMEM((2, depth, 128, 256), F32),
                pltpu.VMEM((2, rows, 256), F32),
                pltpu.VMEM((cols // 2, 2, rows, 256), F32),
                pltpu.VMEM((2 * rows, 128), jnp.int32),
                pltpu.VMEM((256, 256), F32),
                pltpu.VMEM((256, 256), F32),
                pltpu.VMEM((256, 256), F32),
                pltpu.VMEM((cols, 8, 2 * rows), F32),
                pltpu.VMEM((depth, 4, 128), F32),
                dma((5,)),
                dma((4,)),
                dma((4,)),
                dma((2, depth // 2 + 1)),
                dma((2, depth // 2 + 1)),
                dma((depth,)),
                dma((depth,)),
                dma((cols // 2,)),
                dma((cols // 2,)),
                dma,
                dma,
                dma((cols,)),
                dma((cols,)),
                dma((depth,)),
                dma((depth,)),
                pltpu.SemaphoreType.REGULAR((2,)),
            ],
            compiler_params=pltpu.CompilerParams(
                collective_id=0, has_side_effects=True, vmem_limit_bytes=48 * 1024 * 1024
            ),
        )(weights, codebook, assign, chol_upper, inv_blocks)
    )


def solution(mesh):
    return jax.shard_map(
        local,
        mesh=mesh,
        in_specs=(
            P("ea", "row", "col"),
            P("ea", "col", None, None),
            P("ea", "row", "col"),
            P("ea", "row", "col"),
            P("ea", "col", None, None),
        ),
        out_specs=(P("ea", "row", "col"), P("ea", "row"), P("ea", "col", None)),
        check_vma=False,
    )
```

time: 413 us -> 77.8 us (0.19)
  blocking collectives: 219 us -> 0 us
  local copies, waits for them, and re-layouts: 99.5 us -> 5.8 us
  Pallas kernels: 0 us -> 71 us
  other arithmetic: 58.6 us -> 0 us
  starting transfers between devices: 26.8 us -> 0 us
    all_gather x16 -> x0, blocking collectives: 206 us -> none  [picked_2(): lax.all_gather(value, axis)]
    gather x3 -> x0, local copies, waits for them, and re-layouts: 95.9 us -> none  [the longest x2 48 us: select(): jnp.take(rows_table[0], indices)]
    pallas_call x0 -> x1, Pallas kernels: none -> 71 us  [local(): pl.pallas_call(functools.partial(kernel, depth, cols), out_shape=(jax.Sha...]
    unnamed x4 -> x0, other arithmetic: 57.4 us -> none
    all_to_all x2 -> x0, starting transfers between devices: 26.8 us -> none  [sent_to_all(): return lax.all_to_all(copies, axis, split_axis=0, concat_axis=0, tiled=True)]
    psum x1 -> x0, blocking collectives: 13 us -> none  [local(): row_loss = lax.psum(jnp.sum(errors * errors, axis=2), 'col')]
    unnamed x15 -> x13, local copies, waits for them, and re-layouts: 0.12 us -> 5.8 us
  transfers between devices with their start and end apart: 2 -> 0, of which waited for: 0 -> 0; matrix products, arithmetic and copies ran while one was open for 24% -> 0% of each run, Pallas kernels for 0% -> 0%
where the time goes in v1:
time: 77.8 us; the launch traced here: 77.5 us
  Pallas kernels  71 us (91%)
  local copies, waits for them, and re-layouts  5.8 us (7%)
    pallas_call x1, Pallas kernels, local(): pl.pallas_call(functools.partial(kernel, depth, cols), out_shape=(jax.Sha...  71 us
    unnamed x13, local copies, waits for them, and re-layouts  5.8 us

profile of v1, /device:TPU:7, one launch (start us, length us, event | category | flops | bytes accessed | tf_op | source)
XLA Modules:
  0.0 77.5 jit_solution(5874390885285112483)
XLA Ops:
  0.6 0.0 copy-start
  0.6 0.9 %copy-done = f32[1,128,256]{2,1,0:T(8,128)S(1)} copy-done((f32[1,128,256]{2,1,0:T(8,128)S(1)}, f32[1,128,256]{2,1,0:T(8,128)}, u32[]{:S(2)}) %copy-start) | copy-done | bytes 131096
  1.5 0.0 copy-start.1
  1.5 0.9 %copy-done.1 = f32[1,2,128,128]{3,2,1,0:T(8,128)S(1)} copy-done((f32[1,2,128,128]{3,2,1,0:T(8,128)S(1)}, f32[1,2,128,128]{3,2,1,0:T(8,128)}, u32[]{:S(2)}) %copy-start.1) | copy-done | bytes 131096
  2.4 0.0 copy-start.2
  2.4 0.8 %copy-done.2 = f32[1,64,256]{2,1,0:T(8,128)S(1)} copy-done((f32[1,64,256]{2,1,0:T(8,128)S(1)}, f32[1,64,256]{2,1,0:T(8,128)}, u32[]{:S(2)}) %copy-start.2) | copy-done | bytes 65560
  3.3 0.0 copy-start.3
  3.3 0.8 copy-done.3
  4.0 0.0 copy-start.4
  4.0 0.7 copy-done.4
  4.7 71.0 %shard_map.76 = (f32[1,64,256]{2,1,0:T(8,128)S(1)}, f32[1,64]{1,0:T(1,128)S(1)}, f32[1,2,256]{2,1,0:T(2,128)S(1)}) custom-call(f32[1,64,256]{2,1,0:T(8,128)S(1)} %copy-done.2, f32[1,2,2,256]{3,2,1,0:T(2,128)S(1)} %copy-done.4, s32[1,64,128]{2,1,0:T(8,128)S(1)} %copy-done.3, f32[1,128,256]{2,1,0:T(8,128)S(1)} %copy-done, f32[1,2,128,128]{3,2,1,0:T(8,128)S(1)} %copy-done.1), custom_call_target="tpu_custom_call" | custom-call | tf_op jit(solution)/shard_map/pallas_call | solution.py:345
  75.8 0.6 copy.11
  76.4 0.5 copy.12
  76.9 0.6 copy.13
Async XLA Ops:
  0.6 0.9 %copy-start = (f32[1,128,256]{2,1,0:T(8,128)S(1)}, f32[1,128,256]{2,1,0:T(8,128)}, u32[]{:S(2)}) copy-start(f32[1,128,256]{2,1,0:T(8,128)} %u_hbm.1) | copy-start | bytes 393220
  1.5 0.9 %copy-start.1 = (f32[1,2,128,128]{3,2,1,0:T(8,128)S(1)}, f32[1,2,128,128]{3,2,1,0:T(8,128)}, u32[]{:S(2)}) copy-start(f32[1,2,128,128]{3,2,1,0:T(8,128)} %i_hbm.1) | copy-start | bytes 393220
  2.4 0.8 %copy-start.2 = (f32[1,64,256]{2,1,0:T(8,128)S(1)}, f32[1,64,256]{2,1,0:T(8,128)}, u32[]{:S(2)}) copy-start(f32[1,64,256]{2,1,0:T(8,128)} %w_hbm.1) | copy-start | bytes 196612
  3.3 0.8 copy-start.3
  4.0 0.7 copy-start.4
